TPU v7x, 32 devices: a whole 2x2x4 slice. The times are simulated.
32 devices in a mesh: dp: 2 (over x), row: 4 (over z), col: 4 (over y, core).
Axes of the slice: x: 2, y: 2, z: 4, core: 2. Of those that a mesh axis runs over, the one named last changes fastest.
Arguments:
- expand_gradient: bfloat16 [2, 4096, 5120], P('dp', 'row', 'col'), may hold values from -24 to 24, as said below
- expand_master: float32 [4096, 5120], P(('row', 'dp'), 'col'), may hold values from -0.12 to 0.12
- expand_rows: float32 [4096], P(('row', 'dp')), may hold values from 0.01 to 1
- expand_columns: float32 [5120], P('col'), may hold values from 0.01 to 1
- contract_gradient: bfloat16 [2, 5120, 4096], P('dp', 'row', 'col'), may hold values from -24 to 24, as said below
- contract_master: float32 [5120, 4096], P(('row', 'dp'), 'col'), may hold values from -0.12 to 0.12
- contract_rows: float32 [5120], P(('row', 'dp')), may hold values from 0.01 to 1
- contract_columns: float32 [4096], P('col'), may hold values from 0.01 to 1
- attend_gradient: bfloat16 [2, 4096, 4096], P('dp', 'row', 'col'), may hold values from -24 to 24, as said below
- attend_master: float32 [4096, 4096], P(('row', 'dp'), 'col'), may hold values from -0.12 to 0.12
- attend_rows: float32 [4096], P(('row', 'dp')), may hold values from 0.01 to 1
- attend_columns: float32 [4096], P('col'), may hold values from 0.01 to 1
Outputs:
- expand_updated: float32 [4096, 5120], P(('row', 'dp'), 'col')
- expand_weights: bfloat16 [4096, 5120], P('row', 'col')
- expand_rows_next: float32 [4096], P(('row', 'dp'))
- expand_columns_next: float32 [5120], P('col')
- expand_step: float32 [4096, 5120], P(('row', 'dp'), 'col')
- contract_updated: float32 [5120, 4096], P(('row', 'dp'), 'col')
- contract_weights: bfloat16 [5120, 4096], P('row', 'col')
- contract_rows_next: float32 [5120], P(('row', 'dp'))
- contract_columns_next: float32 [4096], P('col')
- contract_step: float32 [5120, 4096], P(('row', 'dp'), 'col')
- attend_updated: float32 [4096, 4096], P(('row', 'dp'), 'col')
- attend_weights: bfloat16 [4096, 4096], P('row', 'col')
- attend_rows_next: float32 [4096], P(('row', 'dp'))
- attend_columns_next: float32 [4096], P('col')
- attend_step: float32 [4096, 4096], P(('row', 'dp'), 'col')
Inputs may be any that keep to these rules, and one draw needn't show every extreme that they name: `expand_gradient`: each replica's gradient, of any scale from entry to entry. `contract_gradient`: each replica's gradient, of any scale from entry to entry. `attend_gradient`: each replica's gradient, of any scale from entry to entry.
All inputs are finite; a program needn't handle non-finite values.
Results may differ from a plain program's by a relative error of at most 0.0004.
Values may be sent and summed in bfloat16 or wider, within the bound.
A program may use at most 128 MiB of HBM per device.

v0:
```python
import jax
import jax.numpy as jnp
from jax import lax
from jax.sharding import PartitionSpec as P

tiny_square = 1e-30
decay_rate = 0.9
learn_rate = 0.01


def finish(update_raw, clip_total, master, full_size):
    clip_scale = jnp.maximum(1.0, jnp.sqrt(clip_total / full_size))
    step_taken = update_raw / clip_scale
    updated = master - learn_rate * step_taken
    weights = lax.all_gather(updated.astype(jnp.bfloat16), "dp", axis=0, tiled=True)
    return (updated, weights, step_taken)


def reduce_gradient(gradient, dp_count):
    received = lax.all_to_all(gradient, "dp", split_axis=1, concat_axis=0, tiled=True)
    summed = jnp.sum(received.astype(jnp.float32), axis=0)
    return summed / dp_count


def body(
    expand_gradient,
    expand_master,
    expand_rows,
    expand_columns,
    contract_gradient,
    contract_master,
    contract_rows,
    contract_columns,
    attend_gradient,
    attend_master,
    attend_rows,
    attend_columns,
):
    groups = (
        (expand_gradient, expand_master, expand_rows, expand_columns),
        (contract_gradient, contract_master, contract_rows, contract_columns),
        (attend_gradient, attend_master, attend_rows, attend_columns),
    )
    dp_count = lax.axis_size("dp")
    col_count = lax.axis_size("col")
    split_count = dp_count * lax.axis_size("row")
    means = []
    for gradient, master, row_stat, column_stat in groups:
        means.append(reduce_gradient(gradient, dp_count))
    squares = [mean_grad * mean_grad + tiny_square for mean_grad in means]
    row_parts = [jnp.sum(square_block, axis=1) for square_block in squares]
    column_parts = [jnp.sum(square_block, axis=0) for square_block in squares]
    heights = [mean_grad.shape[0] * split_count for mean_grad in means]
    widths = [mean_grad.shape[1] * col_count for mean_grad in means]
    outputs = []
    for which in range(3):
        row_total = lax.psum(row_parts[which], "col")
        rows_next = decay_rate * groups[which][2] + (1.0 - decay_rate) * row_total / widths[which]
        column_total, rows_sum = lax.psum((column_parts[which], jnp.sum(rows_next)), ("dp", "row"))
        columns_next = (
            decay_rate * groups[which][3] + (1.0 - decay_rate) * column_total / heights[which]
        )
        row_mean = rows_sum / heights[which]
        update_raw = means[which] * jnp.sqrt(
            row_mean / (rows_next[:, None] * columns_next[None, :])
        )
        clip_total = lax.psum(jnp.sum(update_raw * update_raw), ("dp", "row", "col"))
        updated, weights, step_taken = finish(
            update_raw, clip_total, groups[which][1], heights[which] * widths[which]
        )
        outputs.extend([updated, weights, rows_next, columns_next, step_taken])
    return tuple(outputs)


def solution(mesh):
    return jax.shard_map(
        body,
        mesh=mesh,
        in_specs=(
            P("dp", "row", "col"),
            P(("row", "dp"), "col"),
            P(("row", "dp")),
            P("col"),
            P("dp", "row", "col"),
            P(("row", "dp"), "col"),
            P(("row", "dp")),
            P("col"),
            P("dp", "row", "col"),
            P(("row", "dp"), "col"),
            P(("row", "dp")),
            P("col"),
        ),
        out_specs=(
            P(("row", "dp"), "col"),
            P("row", "col"),
            P(("row", "dp")),
            P("col"),
            P(("row", "dp"), "col"),
            P(("row", "dp"), "col"),
            P("row", "col"),
            P(("row", "dp")),
            P("col"),
            P(("row", "dp"), "col"),
            P(("row", "dp"), "col"),
            P("row", "col"),
            P(("row", "dp")),
            P("col"),
            P(("row", "dp"), "col"),
        ),
        check_vma=False,
    )
```

profile of v0, /device:TPU:0, one launch (start us, length us, event | category | flops | bytes accessed | tf_op | source)
XLA Modules:
  0.0 387.2 jit_solution(6910142270513207531)
XLA Ops:
  7.2 6.8 %copy.41 = bf16[1,1024,1024]{2,0,1:T(2,128)(2,1)} copy(bf16[1,1024,1024]{2,1,0:T(8,128)(2,1)} %param.20) | data formatting | bytes 4194304 | tf_op args[8]
  14.4 12.8 %reduce.2 = bf16[1024,1024]{1,0:T(8,128)(2,1)S(1)} reduce(bf16[1024,1,1024]{2,1,0:T(2,128)(2,1)} %bitcast.22, bf16[]{:T(256)} %broadcast.37), dimensions={1}, to_apply=%bitcast.17.reduce_sub_computation | reduce | bytes 4194306
  27.2 2.5 reshape.58
  29.7 5.5 %all-to-all-start.2 = ((bf16[2,2,262144]{2,1,0:T(2,128)(2,1)}), bf16[2,2,262144]{2,1,0:T(2,128)(2,1)}, u32[]{:S(2)}, u32[]{:S(2)}) async-start(bf16[2,2,262144]{2,1,0:T(2,128)(2,1)} %reshape.58), calls=%async_computation.2 | async-start | bytes 4194304 | tf_op jit(solution)/shard_map/all_to_all | solution.py:20
  35.2 6.4 %copy.40 = bf16[1,1024,1280]{2,0,1:T(2,128)(2,1)} copy(bf16[1,1024,1280]{2,1,0:T(8,128)(2,1)S(1)} %copy-done.4) | data formatting | bytes 5242880 | tf_op args[0]
  41.6 26.6 %reduce = bf16[1024,1280]{1,0:T(8,128)(2,1)S(1)} reduce(bf16[1024,1,1280]{2,1,0:T(2,128)(2,1)} %bitcast.21, bf16[]{:T(256)} %broadcast.37), dimensions={1}, to_apply=%bitcast.16.reduce_sub_computation | reduce | bytes 5242882
  68.2 1.8 reshape.54
  70.0 5.8 %all-to-all-start = ((bf16[2,2,327680]{2,1,0:T(2,128)(2,1)}), bf16[2,2,327680]{2,1,0:T(2,128)(2,1)}, u32[]{:S(2)}, u32[]{:S(2)}) async-start(bf16[2,2,327680]{2,1,0:T(2,128)(2,1)} %reshape.54), calls=%async_computation | async-start | bytes 5242880 | tf_op jit(solution)/shard_map/all_to_all | solution.py:20
  75.9 18.2 %copy.39 = bf16[1,1280,1024]{2,0,1:T(2,128)(2,1)} copy(bf16[1,1280,1024]{2,1,0:T(8,128)(2,1)S(1)} %copy-done.5) | data formatting | bytes 5242880 | tf_op args[4]
  94.1 15.6 %reduce.1 = bf16[1280,1024]{1,0:T(8,128)(2,1)S(1)} reduce(bf16[1280,1,1024]{2,1,0:T(2,128)(2,1)} %bitcast.18, bf16[]{:T(256)} %broadcast.37), dimensions={1}, to_apply=%bitcast.15.reduce_sub_computation | reduce | bytes 5242882
  109.6 3.0 reshape.56
  112.6 4.1 %all-to-all-start.1 = ((bf16[2,2,327680]{2,1,0:T(2,128)(2,1)}), bf16[2,2,327680]{2,1,0:T(2,128)(2,1)S(1)}, u32[]{:S(2)}, u32[]{:S(2)}) async-start(bf16[2,2,327680]{2,1,0:T(2,128)(2,1)} %reshape.56), calls=%async_computation.1 | async-start | bytes 5242880 | tf_op jit(solution)/shard_map/all_to_all | solution.py:20
  116.9 4.3 %reshape.59 = bf16[1024,1,1024]{2,1,0:T(2,128)(2,1)} reshape(bf16[2,2,262144]{2,1,0:T(2,128)(2,1)} %all-to-all-done.2) | data formatting | bytes 4194304
  121.2 3.0 copy.35
  126.5 5.1 %reshape.55 = bf16[1024,1,1280]{2,1,0:T(2,128)(2,1)} reshape(bf16[2,2,327680]{2,1,0:T(2,128)(2,1)} %all-to-all-done) | data formatting | bytes 5242880
  131.5 2.9 copy.31
  137.0 11.3 %all-to-all-done.1 = bf16[2,2,327680]{2,1,0:T(2,128)(2,1)S(1)} async-done(((bf16[2,2,327680]{2,1,0:T(2,128)(2,1)}), bf16[2,2,327680]{2,1,0:T(2,128)(2,1)S(1)}, u32[]{:S(2)}, u32[]{:S(2)}) %all-to-all-start.1) | async-done | bytes 2621472 | tf_op jit(solution)/shard_map/all_to_all | solution.py:20
  148.3 3.7 reshape.57
  152.1 3.5 copy.33
  156.8 6.2 %all-reduce.2 = (f32[512]{0:T(512)S(1)}, f32[640]{0:T(1024)S(1)}, f32[512]{0:T(512)S(1)}) all-reduce(f32[512]{0:T(512)S(1)} %get-tuple-element.17, f32[640]{0:T(1024)S(1)} %get-tuple-element.15, f32[512]{0:T(512)S(1)} %get-tuple-element.19), channel_id=1, replica_groups=mesh['dp'=2,'row'=4,'col'=4] {'col'}, use_global_device_ids=true, to_apply=%region_2.0 | all-reduce | flops 1664 | bytes 13312 | tf_op jit(solution)/shard_map/psum | solution.py:57
  164.2 38.0 %all-reduce.1 = (f32[1280]{0:T(1024)S(1)}, f32[]{:T(128)}, f32[1024]{0:T(1024)S(1)}, f32[]{:T(128)}, f32[1024]{0:T(1024)S(1)}, /*index=5*/f32[]{:T(128)}) all-reduce(f32[1280]{0:T(1024)S(1)} %get-tuple-element.18, f32[]{:T(128)} %get-tuple-element.48, ...), channel_id=1, replica_groups=mesh['dp'=2,'row'=4,'col'=4] {'dp','row'}, use_global_device_ids=true, to_apply=%region_6.0 | all-reduce | flops 3331 | bytes 26648 | tf_op jit(solution)/shard_map/psum | solution.py:59
  204.2 3.8 multiply_reduce_fusion.1
  208.0 2.3 multiply_reduce_fusion
  210.3 2.0 multiply_reduce_fusion.2
  212.2 37.2 %all-reduce = (f32[]{:T(128)}, f32[]{:T(128)}, f32[]{:T(128)}) all-reduce(f32[]{:T(128)} %multiply_reduce_fusion.1, f32[]{:T(128)} %multiply_reduce_fusion, f32[]{:T(128)} %multiply_reduce_fusion.2), channel_id=1, replica_groups=mesh['dp'=2,'row'=4,'col'=4] {'dp','row','col'}, use_global_device_ids=true, to_apply=%region_8.0 | all-reduce | flops 3 | bytes 24 | tf_op jit(solution)/shard_map/psum | solution.py:67
  250.2 5.9 %fusion.6 = (bf16[512,1024]{1,0:T(8,128)(2,1)}, f32[512,1024]{1,0:T(8,128)}, f32[512,1024]{1,0:T(8,128)}) fusion(f32[512,1024]{1,0:T(8,128)} %param.21, f32[]{:T(128)S(6)} %max.11, f32[1024]{0:T(1024)S(1)} %multiply_add_fusion.4, f32[512]{0:T(512)S(1)} %get-tuple-element.77, f32[]{:T(128)S(6)} %div.136, f32[512,1024]{1,0:T(8,128)} %copy-done.1), kind=kLoop, calls=%fused_computation.30 | loop fusion | flops 4194304 | bytes 9443336 | tf_op jit(solution)/shard_map/convert_element_type | solution.py:15
  256.9 6.7 %fusion.8 = (bf16[512,1280]{1,0:T(8,128)(2,1)}, f32[512,1280]{1,0:T(8,128)}, f32[512,1280]{1,0:T(8,128)}) fusion(f32[512,1280]{1,0:T(8,128)} %param.13, f32[]{:T(128)S(6)} %max.9, f32[1280]{0:T(1024)S(1)} %multiply_add_fusion.3, f32[512]{0:T(512)S(1)} %get-tuple-element.67, f32[]{:T(128)S(6)} %div.112, f32[512,1280]{1,0:T(8,128)} %copy-done), kind=kLoop, calls=%fused_computation.32 | loop fusion | flops 5242880 | bytes 11803656 | tf_op jit(solution)/shard_map/convert_element_type | solution.py:15
  264.3 6.3 %fusion.7 = (bf16[640,1024]{1,0:T(8,128)(2,1)}, f32[640,1024]{1,0:T(8,128)}, f32[640,1024]{1,0:T(8,128)}) fusion(f32[640,1024]{1,0:T(8,128)} %param.17, f32[]{:T(128)S(6)} %max.10, f32[1024]{0:T(1024)S(1)} %multiply_add_fusion.5, f32[640]{0:T(1024)S(1)} %get-tuple-element.72, f32[]{:T(128)S(6)} %div.124, f32[640,1024]{1,0:T(8,128)S(1)} %convert_reduce_fusion), kind=kLoop, calls=%fused_computation.31 | loop fusion | flops 5242880 | bytes 11803144 | tf_op jit(solution)/shard_map/convert_element_type | solution.py:15
  270.6 20.2 %all-gather.8.cloned.1.call-done = bf16[1024,1024]{1,0:T(8,128)(2,1)} async-done(((bf16[512,1024]{1,0:T(8,128)(2,1)}), bf16[1024,1024]{1,0:T(8,128)(2,1)}) %all-gather.8.cloned.1.call-update) | async-done | bytes 2097168 | tf_op jit(solution)/shard_map/all_gather | solution.py:15
  290.7 41.1 %all-gather.4.cloned.1.call-done = bf16[1024,1280]{1,0:T(8,128)(2,1)} async-done(((bf16[512,1280]{1,0:T(8,128)(2,1)}), bf16[1024,1280]{1,0:T(8,128)(2,1)}) %all-gather.4.cloned.1.call-update) | async-done | bytes 2621456 | tf_op jit(solution)/shard_map/all_gather | solution.py:15
  331.9 41.2 %all-gather.6.cloned.1.call-done = bf16[1280,1024]{1,0:T(8,128)(2,1)} async-done(((bf16[640,1024]{1,0:T(8,128)(2,1)}), bf16[1280,1024]{1,0:T(8,128)(2,1)}) %all-gather.6.cloned.1.call-update) | async-done | bytes 2621456 | tf_op jit(solution)/shard_map/all_gather | solution.py:15
  373.1 3.5 copy.45
  (60 shorter events, 11.9 us)
Async XLA Ops:
  29.7 5.5 %copy-start.4 = (bf16[1,1024,1280]{2,1,0:T(8,128)(2,1)S(1)}, bf16[1,1024,1280]{2,1,0:T(8,128)(2,1)}, u32[]{:S(2)}) copy-start(bf16[1,1024,1280]{2,1,0:T(8,128)(2,1)} %param.12) | copy-start | bytes 7864324
  29.7 40.3 %all-to-all-start.2 = ((bf16[2,2,262144]{2,1,0:T(2,128)(2,1)}), bf16[2,2,262144]{2,1,0:T(2,128)(2,1)}, u32[]{:S(2)}, u32[]{:S(2)}) async-start(bf16[2,2,262144]{2,1,0:T(2,128)(2,1)} %reshape.58), calls=%async_computation.2 | async-start | bytes 4194304 | tf_op jit(solution)/shard_map/all_to_all | solution.py:20
  70.0 5.8 %copy-start.5 = (bf16[1,1280,1024]{2,1,0:T(8,128)(2,1)S(1)}, bf16[1,1280,1024]{2,1,0:T(8,128)(2,1)}, u32[]{:S(2)}) copy-start(bf16[1,1280,1024]{2,1,0:T(8,128)(2,1)} %param.16) | copy-start | bytes 7864324
  70.0 42.6 %all-to-all-start = ((bf16[2,2,327680]{2,1,0:T(2,128)(2,1)}), bf16[2,2,327680]{2,1,0:T(2,128)(2,1)}, u32[]{:S(2)}, u32[]{:S(2)}) async-start(bf16[2,2,327680]{2,1,0:T(2,128)(2,1)} %reshape.54), calls=%async_computation | async-start | bytes 5242880 | tf_op jit(solution)/shard_map/all_to_all | solution.py:20
  112.6 35.7 %all-to-all-start.1 = ((bf16[2,2,327680]{2,1,0:T(2,128)(2,1)}), bf16[2,2,327680]{2,1,0:T(2,128)(2,1)S(1)}, u32[]{:S(2)}, u32[]{:S(2)}) async-start(bf16[2,2,327680]{2,1,0:T(2,128)(2,1)} %reshape.56), calls=%async_computation.1 | async-start | bytes 5242880 | tf_op jit(solution)/shard_map/all_to_all | solution.py:20
  116.8 174.0 %all-gather.8.cloned.1.call-start = ((), (), s32[]{:S(2)}) async-start(), calls=%async_computation.5 | async-start | bytes 3145728 | tf_op jit(solution)/shard_map/all_gather | solution.py:15
  124.7 1.3 copy-start.1
  134.9 1.5 copy-start
  156.2 6.8 %copy-start.14 = (f32[640]{0:T(1024)S(1)}, f32[640]{0:T(1024)}, u32[]{:S(2)}) copy-start(f32[640]{0:T(1024)} %param.18) | copy-start | bytes 7684
  156.2 7.4 %copy-start.17 = (f32[512]{0:T(512)S(1)}, f32[512]{0:T(512)}, u32[]{:S(2)}) copy-start(f32[512]{0:T(512)} %param.22) | copy-start | bytes 6148
  156.2 7.4 %copy-start.18 = (f32[512]{0:T(512)S(1)}, f32[512]{0:T(512)}, u32[]{:S(2)}) copy-start(f32[512]{0:T(512)} %param.14) | copy-start | bytes 6148
  156.2 47.3 %copy-start.13 = (f32[1280]{0:T(1024)S(1)}, f32[1280]{0:T(1024)}, u32[]{:S(2)}) copy-start(f32[1280]{0:T(1024)} %param.15) | copy-start | bytes 15364
  156.2 47.3 %copy-start.15 = (f32[1024]{0:T(1024)S(1)}, f32[1024]{0:T(1024)}, u32[]{:S(2)}) copy-start(f32[1024]{0:T(1024)} %param.19) | copy-start | bytes 12292
  156.2 48.0 %copy-start.16 = (f32[1024]{0:T(1024)S(1)}, f32[1024]{0:T(1024)}, u32[]{:S(2)}) copy-start(f32[1024]{0:T(1024)} %param.23) | copy-start | bytes 12292
  163.6 100.7 %copy-start.9 = (f32[640]{0:T(1024)}, f32[640]{0:T(1024)S(1)}, u32[]{:S(2)}) copy-start(f32[640]{0:T(1024)S(1)} %get-tuple-element.72) | copy-start | bytes 7684
  164.2 86.0 %copy-start.11 = (f32[512]{0:T(512)}, f32[512]{0:T(512)S(1)}, u32[]{:S(2)}) copy-start(f32[512]{0:T(512)S(1)} %get-tuple-element.77) | copy-start | bytes 6148
  164.2 92.6 %copy-start.12 = (f32[512]{0:T(512)}, f32[512]{0:T(512)S(1)}, u32[]{:S(2)}) copy-start(f32[512]{0:T(512)S(1)} %get-tuple-element.67) | copy-start | bytes 6148
  203.5 53.3 %copy-start.7 = (f32[1280]{0:T(1024)}, f32[1280]{0:T(1024)S(1)}, u32[]{:S(2)}) copy-start(f32[1280]{0:T(1024)S(1)} %multiply_add_fusion.3) | copy-start | bytes 15364
  203.5 60.7 %copy-start.10 = (f32[1024]{0:T(1024)}, f32[1024]{0:T(1024)S(1)}, u32[]{:S(2)}) copy-start(f32[1024]{0:T(1024)S(1)} %multiply_add_fusion.5) | copy-start | bytes 12292
  204.2 46.0 %copy-start.8 = (f32[1024]{0:T(1024)}, f32[1024]{0:T(1024)S(1)}, u32[]{:S(2)}) copy-start(f32[1024]{0:T(1024)S(1)} %multiply_add_fusion.4) | copy-start | bytes 12292
  204.2 6.1 %copy-start.2 = (f32[512,1024]{1,0:T(8,128)S(1)}, f32[512,1024]{1,0:T(8,128)}, u32[]{:S(2)}) copy-start(f32[512,1024]{1,0:T(8,128)} %copy-done.1) | copy-start | bytes 6291460
  256.1 75.8 %all-gather.4.cloned.1.call-start = ((), (), s32[]{:S(2)}) async-start(), calls=%async_computation.3 | async-start | bytes 3932160 | tf_op jit(solution)/shard_map/all_gather | solution.py:15
  263.5 109.5 %all-gather.6.cloned.1.call-start = ((), (), s32[]{:S(2)}) async-start(), calls=%async_computation.4 | async-start | bytes 3932160 | tf_op jit(solution)/shard_map/all_gather | solution.py:15
  373.1 3.6 copy-start.3
  376.6 2.5 copy-start.6
Sparse Core Ops, SparseCore 0:
  256.2 34.4 all-gather.7
  292.9 38.9 all-gather.3
  334.0 38.9 all-gather.5
where the time goes:
time: 393 us; the launch traced here: 387 us
  waiting for transfers between devices  114 us (29%)
  other arithmetic  86.1 us (22%)
  blocking collectives  81.4 us (21%)
  local copies, waits for them, and re-layouts  71.9 us (18%)
  between operations  18.3 us (5%)
  starting transfers between devices  15.7 us (4%)
    all_gather x3, waiting for transfers between devices, finish(): lax.all_gather(updated.astype(jnp.bfloat16), 'dp', axis=0, tiled=True)  102 us
    unnamed x51, local copies, waits for them, and re-layouts  62.5 us
    unnamed x3, other arithmetic  55 us
    psum x1, blocking collectives, body(): lax.psum((column_parts[which], jnp.sum(rows_next)), ('dp', 'row'))  38 us
    psum x1, blocking collectives, body(): lax.psum(jnp.sum(update_raw * update_raw), ('dp', 'row', 'col'))  37.2 us
    convert_element_type x3, other arithmetic, finish(): updated.astype(jnp.bfloat16)  18.8 us
    all_to_all x3, starting transfers between devices, reduce_gradient(): lax.all_to_all(gradient, 'dp', split_axis=1, concat_axis=0, tiled=True)  15.4 us
    all_to_all x3, waiting for transfers between devices, reduce_gradient(): lax.all_to_all(gradient, 'dp', split_axis=1, concat_axis=0, tiled=True)  11.3 us
  transfers between devices with their start and end apart: 6, of which 4 were waited for; matrix products, arithmetic and copies ran while one was open for 26% of the time, Pallas kernels for 0%

commit v1 on v0

--- a/solution.py
+++ b/solution.py
@@ -17,7 +17,10 @@
 
 
 def reduce_gradient(gradient, dp_count):
-    received = lax.all_to_all(gradient, "dp", split_axis=1, concat_axis=0, tiled=True)
+    received = jnp.concatenate(
+        lax.all_to_all(jnp.stack(jnp.split(gradient, lax.axis_size("dp"), axis=1)), "dp", 0, 0),
+        axis=0,
+    )
     summed = jnp.sum(received.astype(jnp.float32), axis=0)
     return summed / dp_count
 

time: 393 us -> 345 us (0.88); the launches traced: 387 us -> 344 us
  waiting for transfers between devices: 114 us -> 174 us
  local copies, waits for them, and re-layouts: 71.9 us -> 18.1 us
  other arithmetic: 86.1 us -> 40.1 us
    all_to_all x3, waiting for transfers between devices: 11.3 us -> 71.9 us  [reduce_gradient(): lax.all_to_all(jnp.stack(jnp.split(gradient, lax.axis_size('dp'), axis=1)...]
    unnamed x3 -> x0, other arithmetic: 55 us -> none
    unnamed x51 -> x43, local copies, waits for them, and re-layouts: 62.5 us -> 12.5 us
    all_to_all x3 -> x0, local copies, waits for them, and re-layouts: 9.41 us -> none  [reduce_gradient(): lax.all_to_all(gradient, 'dp', split_axis=1, concat_axis=0, tiled=True)]
    another operation x0 -> x3, local copies, waits for them, and re-layouts: none -> 5.54 us  [reduce_gradient(): jnp.stack(jnp.split(gradient, lax.axis_size('dp'), axis=1))]
    another operation x0 -> x3, other arithmetic: none -> 4.94 us  [reduce_gradient(): jnp.stack(jnp.split(gradient, lax.axis_size('dp'), axis=1))]
    reduce_sum x3, other arithmetic: 1.47 us -> 5.43 us  [reduce_gradient(): summed = jnp.sum(received.astype(jnp.float32), axis=0)]
  transfers between devices with their start and end apart: 6 -> 6, of which waited for: 4 -> 6; matrix products, arithmetic and copies ran while one was open for 26% -> 7% of each run, Pallas kernels for 0% -> 0%
where the time goes in v1:
time: 345 us; the launch traced here: 344 us
  waiting for transfers between devices  174 us (50%)
  blocking collectives  80.5 us (23%)
  other arithmetic  40.1 us (12%)
  local copies, waits for them, and re-layouts  18.1 us (5%)
  between operations  18 us (5%)
  starting transfers between devices  13.2 us (4%)
    all_gather x3, waiting for transfers between devices, finish(): lax.all_gather(updated.astype(jnp.bfloat16), 'dp', axis=0, tiled=True)  102 us
    all_to_all x3, waiting for transfers between devices, reduce_gradient(): lax.all_to_all(jnp.stack(jnp.split(gradient, lax.axis_size('dp'), axis=1)...  71.9 us
    psum x1, blocking collectives, body(): lax.psum(jnp.sum(update_raw * update_raw), ('dp', 'row', 'col'))  37.6 us
    psum x1, blocking collectives, body(): lax.psum((column_parts[which], jnp.sum(rows_next)), ('dp', 'row'))  37.2 us
    convert_element_type x3, other arithmetic, finish(): updated.astype(jnp.bfloat16)  19 us
    all_to_all x3, starting transfers between devices, reduce_gradient(): lax.all_to_all(jnp.stack(jnp.split(gradient, lax.axis_size('dp'), axis=1)...  13.1 us
    unnamed x43, local copies, waits for them, and re-layouts  12.5 us
    reduce_sum x3, other arithmetic, body(): jnp.sum(update_raw * update_raw)  8 us
  transfers between devices with their start and end apart: 6, of which 6 were waited for; matrix products, arithmetic and copies ran while one was open for 7% of the time, Pallas kernels for 0%

profile of v1, /device:TPU:0, one launch (start us, length us, event | category | flops | bytes accessed | tf_op | source)
XLA Modules:
  0.0 344.4 jit_solution(3970008219703649295)
XLA Ops:
  7.2 1.7 slice_bitcast_fusion.5
  8.9 1.5 pad_maximum_fusion.2
  10.4 4.2 %all-to-all-start.2 = ((bf16[2,1,512,1024]{3,2,1,0:T(8,128)(2,1)}), bf16[2,1,512,1024]{3,2,1,0:T(8,128)(2,1)S(1)}, u32[]{:S(2)}, u32[]{:S(2)}) async-start(bf16[2,1,512,1024]{3,2,1,0:T(8,128)(2,1)} %pad_maximum_fusion.2), calls=%async_computation.2 | async-start | bytes 4194304 | tf_op jit(solution)/shard_map/all_to_all | solution.py:21
  14.6 1.9 slice_bitcast_fusion.3
  16.5 1.7 pad_maximum_fusion
  18.2 22.3 %all-to-all-done.2 = bf16[2,1,512,1024]{3,2,1,0:T(8,128)(2,1)S(1)} async-done(((bf16[2,1,512,1024]{3,2,1,0:T(8,128)(2,1)}), bf16[2,1,512,1024]{3,2,1,0:T(8,128)(2,1)S(1)}, u32[]{:S(2)}, u32[]{:S(2)}) %all-to-all-start.2) | async-done | bytes 2097184 | tf_op jit(solution)/shard_map/all_to_all | solution.py:21
  40.5 1.3 copy-done.5
  41.8 3.9 %all-to-all-start = ((bf16[2,1,512,1280]{3,2,1,0:T(8,128)(2,1)}), bf16[2,1,512,1280]{3,2,1,0:T(8,128)(2,1)S(1)}, u32[]{:S(2)}, u32[]{:S(2)}) async-start(bf16[2,1,512,1280]{3,2,1,0:T(8,128)(2,1)} %pad_maximum_fusion), calls=%async_computation | async-start | bytes 5242880 | tf_op jit(solution)/shard_map/all_to_all | solution.py:21
  45.7 2.0 slice_bitcast_fusion.1
  47.6 1.7 pad_maximum_fusion.1
  49.3 26.5 %all-to-all-done = bf16[2,1,512,1280]{3,2,1,0:T(8,128)(2,1)S(1)} async-done(((bf16[2,1,512,1280]{3,2,1,0:T(8,128)(2,1)}), bf16[2,1,512,1280]{3,2,1,0:T(8,128)(2,1)S(1)}, u32[]{:S(2)}, u32[]{:S(2)}) %all-to-all-start) | async-done | bytes 2621472 | tf_op jit(solution)/shard_map/all_to_all | solution.py:21
  75.8 1.5 copy-done.3
  77.3 5.0 %all-to-all-start.1 = ((bf16[2,1,640,1024]{3,2,1,0:T(8,128)(2,1)}), bf16[2,1,640,1024]{3,2,1,0:T(8,128)(2,1)}, u32[]{:S(2)}, u32[]{:S(2)}) async-start(bf16[2,1,640,1024]{3,2,1,0:T(8,128)(2,1)} %pad_maximum_fusion.1), calls=%async_computation.1 | async-start | bytes 5242880 | tf_op jit(solution)/shard_map/all_to_all | solution.py:21
  82.4 2.4 convert_reduce_fusion.2
  84.8 1.3 copy-done.1
  88.5 23.2 %all-to-all-done.1 = bf16[2,1,640,1024]{3,2,1,0:T(8,128)(2,1)} async-done(((bf16[2,1,640,1024]{3,2,1,0:T(8,128)(2,1)}), bf16[2,1,640,1024]{3,2,1,0:T(8,128)(2,1)}, u32[]{:S(2)}, u32[]{:S(2)}) %all-to-all-start.1) | async-done | bytes 2621472 | tf_op jit(solution)/shard_map/all_to_all | solution.py:21
  111.7 2.6 convert_reduce_fusion
  114.9 5.8 %all-reduce.2 = (f32[512]{0:T(512)S(1)}, f32[640]{0:T(1024)S(1)}, f32[512]{0:T(512)S(1)}) all-reduce(f32[512]{0:T(512)S(1)} %get-tuple-element.17, f32[640]{0:T(1024)S(1)} %get-tuple-element.15, f32[512]{0:T(512)S(1)} %get-tuple-element.19), channel_id=1, replica_groups=mesh['dp'=2,'row'=4,'col'=4] {'col'}, use_global_device_ids=true, to_apply=%region_2.0 | all-reduce | flops 1664 | bytes 13312 | tf_op jit(solution)/shard_map/psum | solution.py:60
  121.9 37.2 %all-reduce.1 = (f32[1280]{0:T(1024)S(1)}, f32[]{:T(128)}, f32[1024]{0:T(1024)S(1)}, f32[]{:T(128)}, f32[1024]{0:T(1024)S(1)}, /*index=5*/f32[]{:T(128)}) all-reduce(f32[1280]{0:T(1024)S(1)} %get-tuple-element.18, f32[]{:T(128)} %get-tuple-element.54, ...), channel_id=1, replica_groups=mesh['dp'=2,'row'=4,'col'=4] {'dp','row'}, use_global_device_ids=true, to_apply=%region_6.0 | all-reduce | flops 3331 | bytes 26648 | tf_op jit(solution)/shard_map/psum | solution.py:62
  161.1 3.8 %multiply_reduce_fusion.1 = f32[]{:T(128)} fusion(f32[1280]{0:T(1024)S(1)} %multiply_add_fusion.3, f32[512]{0:T(512)S(1)} %get-tuple-element.73, f32[]{:T(128)S(6)} %div.112, f32[512,1280]{1,0:T(8,128)} %copy-done), kind=kLoop, calls=%fused_computation.10 | loop fusion | flops 3932159 | bytes 2628616 | tf_op jit(solution)/shard_map/reduce_sum | solution.py:70
  164.9 2.3 multiply_reduce_fusion
  167.2 2.0 multiply_reduce_fusion.2
  169.1 37.6 %all-reduce = (f32[]{:T(128)}, f32[]{:T(128)}, f32[]{:T(128)}) all-reduce(f32[]{:T(128)} %multiply_reduce_fusion.1, f32[]{:T(128)} %multiply_reduce_fusion, f32[]{:T(128)} %multiply_reduce_fusion.2), channel_id=1, replica_groups=mesh['dp'=2,'row'=4,'col'=4] {'dp','row','col'}, use_global_device_ids=true, to_apply=%region_8.0 | all-reduce | flops 3 | bytes 24 | tf_op jit(solution)/shard_map/psum | solution.py:70
  207.4 5.9 %fusion.6 = (bf16[512,1024]{1,0:T(8,128)(2,1)}, f32[512,1024]{1,0:T(8,128)}, f32[512,1024]{1,0:T(8,128)}) fusion(f32[512,1024]{1,0:T(8,128)} %param.21, f32[]{:T(128)S(6)} %max.11, f32[1024]{0:T(1024)S(1)} %multiply_add_fusion.4, f32[512]{0:T(512)S(1)} %get-tuple-element.83, f32[]{:T(128)S(6)} %div.136, f32[512,1024]{1,0:T(8,128)} %copy-done.1), kind=kLoop, calls=%fused_computation.39 | loop fusion | flops 4194304 | bytes 9443336 | tf_op jit(solution)/shard_map/convert_element_type | solution.py:15
  214.1 6.7 %fusion.8 = (bf16[512,1280]{1,0:T(8,128)(2,1)}, f32[512,1280]{1,0:T(8,128)}, f32[512,1280]{1,0:T(8,128)}) fusion(f32[512,1280]{1,0:T(8,128)} %param.13, f32[]{:T(128)S(6)} %max.9, f32[1280]{0:T(1024)S(1)} %multiply_add_fusion.3, f32[512]{0:T(512)S(1)} %get-tuple-element.73, f32[]{:T(128)S(6)} %div.112, f32[512,1280]{1,0:T(8,128)} %copy-done), kind=kLoop, calls=%fused_computation.41 | loop fusion | flops 5242880 | bytes 11803656 | tf_op jit(solution)/shard_map/convert_element_type | solution.py:15
  221.5 6.4 %fusion.7 = (bf16[640,1024]{1,0:T(8,128)(2,1)}, f32[640,1024]{1,0:T(8,128)}, f32[640,1024]{1,0:T(8,128)}) fusion(f32[640,1024]{1,0:T(8,128)} %param.17, f32[]{:T(128)S(6)} %max.10, f32[1024]{0:T(1024)S(1)} %multiply_add_fusion.5, f32[640]{0:T(1024)S(1)} %get-tuple-element.78, f32[]{:T(128)S(6)} %div.124, f32[640,1024]{1,0:T(8,128)S(1)} %convert_reduce_fusion), kind=kLoop, calls=%fused_computation.40 | loop fusion | flops 5242880 | bytes 11803144 | tf_op jit(solution)/shard_map/convert_element_type | solution.py:15
  227.9 20.2 %all-gather.8.cloned.1.call-done = bf16[1024,1024]{1,0:T(8,128)(2,1)} async-done(((bf16[512,1024]{1,0:T(8,128)(2,1)}), bf16[1024,1024]{1,0:T(8,128)(2,1)}) %all-gather.8.cloned.1.call-update) | async-done | bytes 2097168 | tf_op jit(solution)/shard_map/all_gather | solution.py:15
  248.1 41.1 %all-gather.4.cloned.1.call-done = bf16[1024,1280]{1,0:T(8,128)(2,1)} async-done(((bf16[512,1280]{1,0:T(8,128)(2,1)}), bf16[1024,1280]{1,0:T(8,128)(2,1)}) %all-gather.4.cloned.1.call-update) | async-done | bytes 2621456 | tf_op jit(solution)/shard_map/all_gather | solution.py:15
  289.3 41.2 %all-gather.6.cloned.1.call-done = bf16[1280,1024]{1,0:T(8,128)(2,1)} async-done(((bf16[640,1024]{1,0:T(8,128)(2,1)}), bf16[1280,1024]{1,0:T(8,128)(2,1)}) %all-gather.6.cloned.1.call-update) | async-done | bytes 2621456 | tf_op jit(solution)/shard_map/all_gather | solution.py:15
  330.4 3.5 %copy.30 = bf16[1024,1280]{1,0:T(8,128)(2,1)} copy(bf16[1024,1280]{1,0:T(8,128)(2,1)} %all-gather.4.cloned.1.call-done) | data formatting | bytes 5242880
  334.0 1.5 copy.31
  336.5 1.3 copy.32
  (52 shorter events, 5.5 us)
Async XLA Ops:
  10.4 30.1 %all-to-all-start.2 = ((bf16[2,1,512,1024]{3,2,1,0:T(8,128)(2,1)}), bf16[2,1,512,1024]{3,2,1,0:T(8,128)(2,1)S(1)}, u32[]{:S(2)}, u32[]{:S(2)}) async-start(bf16[2,1,512,1024]{3,2,1,0:T(8,128)(2,1)} %pad_maximum_fusion.2), calls=%async_computation.2 | async-start | bytes 4194304 | tf_op jit(solution)/shard_map/all_to_all | solution.py:21
  40.5 1.3 copy-start.5
  41.8 34.0 %all-to-all-start = ((bf16[2,1,512,1280]{3,2,1,0:T(8,128)(2,1)}), bf16[2,1,512,1280]{3,2,1,0:T(8,128)(2,1)S(1)}, u32[]{:S(2)}, u32[]{:S(2)}) async-start(bf16[2,1,512,1280]{3,2,1,0:T(8,128)(2,1)} %pad_maximum_fusion), calls=%async_computation | async-start | bytes 5242880 | tf_op jit(solution)/shard_map/all_to_all | solution.py:21
  75.8 1.5 copy-start.3
  77.3 34.4 %all-to-all-start.1 = ((bf16[2,1,640,1024]{3,2,1,0:T(8,128)(2,1)}), bf16[2,1,640,1024]{3,2,1,0:T(8,128)(2,1)}, u32[]{:S(2)}, u32[]{:S(2)}) async-start(bf16[2,1,640,1024]{3,2,1,0:T(8,128)(2,1)} %pad_maximum_fusion.1), calls=%async_computation.1 | async-start | bytes 5242880 | tf_op jit(solution)/shard_map/all_to_all | solution.py:21
  82.3 165.8 %all-gather.8.cloned.1.call-start = ((), (), s32[]{:S(2)}) async-start(), calls=%async_computation.5 | async-start | bytes 3145728 | tf_op jit(solution)/shard_map/all_gather | solution.py:15
  82.4 4.2 %copy-start.4 = (bf16[2,1,512,1280]{3,2,1,0:T(8,128)(2,1)S(1)}, bf16[2,1,512,1280]{3,2,1,0:T(8,128)(2,1)}, u32[]{:S(2)}) copy-start(bf16[2,1,512,1280]{3,2,1,0:T(8,128)(2,1)} %copy-done.3) | copy-start | bytes 7864324
  84.8 1.3 copy-start.1
  87.0 1.5 copy-start
  114.3 6.4 %copy-start.15 = (f32[640]{0:T(1024)S(1)}, f32[640]{0:T(1024)}, u32[]{:S(2)}) copy-start(f32[640]{0:T(1024)} %param.18) | copy-start | bytes 7684
  114.3 7.0 %copy-start.18 = (f32[512]{0:T(512)S(1)}, f32[512]{0:T(512)}, u32[]{:S(2)}) copy-start(f32[512]{0:T(512)} %param.22) | copy-start | bytes 6148
  114.3 7.0 %copy-start.19 = (f32[512]{0:T(512)S(1)}, f32[512]{0:T(512)}, u32[]{:S(2)}) copy-start(f32[512]{0:T(512)} %param.14) | copy-start | bytes 6148
  114.3 46.0 %copy-start.14 = (f32[1280]{0:T(1024)S(1)}, f32[1280]{0:T(1024)}, u32[]{:S(2)}) copy-start(f32[1280]{0:T(1024)} %param.15) | copy-start | bytes 15364
  114.3 46.1 %copy-start.16 = (f32[1024]{0:T(1024)S(1)}, f32[1024]{0:T(1024)}, u32[]{:S(2)}) copy-start(f32[1024]{0:T(1024)} %param.19) | copy-start | bytes 12292
  114.3 46.7 %copy-start.17 = (f32[1024]{0:T(1024)S(1)}, f32[1024]{0:T(1024)}, u32[]{:S(2)}) copy-start(f32[1024]{0:T(1024)} %param.23) | copy-start | bytes 12292
  121.2 100.2 %copy-start.10 = (f32[640]{0:T(1024)}, f32[640]{0:T(1024)S(1)}, u32[]{:S(2)}) copy-start(f32[640]{0:T(1024)S(1)} %get-tuple-element.78) | copy-start | bytes 7684
  121.9 85.5 %copy-start.12 = (f32[512]{0:T(512)}, f32[512]{0:T(512)S(1)}, u32[]{:S(2)}) copy-start(f32[512]{0:T(512)S(1)} %get-tuple-element.83) | copy-start | bytes 6148
  121.9 92.2 %copy-start.13 = (f32[512]{0:T(512)}, f32[512]{0:T(512)S(1)}, u32[]{:S(2)}) copy-start(f32[512]{0:T(512)S(1)} %get-tuple-element.73) | copy-start | bytes 6148
  160.4 53.7 %copy-start.8 = (f32[1280]{0:T(1024)}, f32[1280]{0:T(1024)S(1)}, u32[]{:S(2)}) copy-start(f32[1280]{0:T(1024)S(1)} %multiply_add_fusion.3) | copy-start | bytes 15364
  160.4 61.1 %copy-start.11 = (f32[1024]{0:T(1024)}, f32[1024]{0:T(1024)S(1)}, u32[]{:S(2)}) copy-start(f32[1024]{0:T(1024)S(1)} %multiply_add_fusion.5) | copy-start | bytes 12292
  161.1 46.3 %copy-start.9 = (f32[1024]{0:T(1024)}, f32[1024]{0:T(1024)S(1)}, u32[]{:S(2)}) copy-start(f32[1024]{0:T(1024)S(1)} %multiply_add_fusion.4) | copy-start | bytes 12292
  161.1 6.1 %copy-start.2 = (f32[512,1024]{1,0:T(8,128)S(1)}, f32[512,1024]{1,0:T(8,128)}, u32[]{:S(2)}) copy-start(f32[512,1024]{1,0:T(8,128)} %copy-done.1) | copy-start | bytes 6291460
  213.3 75.9 %all-gather.4.cloned.1.call-start = ((), (), s32[]{:S(2)}) async-start(), calls=%async_computation.3 | async-start | bytes 3932160 | tf_op jit(solution)/shard_map/all_gather | solution.py:15
  220.8 109.6 %all-gather.6.cloned.1.call-start = ((), (), s32[]{:S(2)}) async-start(), calls=%async_computation.4 | async-start | bytes 3932160 | tf_op jit(solution)/shard_map/all_gather | solution.py:15
  330.4 3.6 %copy-start.6 = (bf16[1280,1024]{1,0:T(8,128)(2,1)S(1)}, bf16[1280,1024]{1,0:T(8,128)(2,1)}, u32[]{:S(2)}) copy-start(bf16[1280,1024]{1,0:T(8,128)(2,1)} %all-gather.6.cloned.1.call-done) | copy-start | bytes 7864324
  334.0 2.5 copy-start.7
Sparse Core Ops, SparseCore 0:
  213.5 34.6 all-gather.7
  250.2 38.9 all-gather.3
  291.4 38.9 all-gather.5
